TPU v7x, 32 devices: a whole 2x2x4 slice. The times are simulated.
32 devices in a mesh: slab: 8 (over y, x, core), det: 4 (over z).
Axes of the slice: x: 2, y: 2, z: 4, core: 2. Of those that a mesh axis runs over, the one named last changes fastest.
Arguments:
- traces: float32 [32, 128, 4096], P(('slab', 'det')), may hold values from -6 to 6
- tables: bfloat16 [32, 256, 2048], P('slab', None, 'det'), may hold values from -0.0625 to 0.0625
- slab_range: int32 [32, 2], P(('slab', 'det')), may hold values from 0 to 7, as said below
- table_slot: int32 [32, 7], P(('slab', 'det')), may hold values from 0 to 3
- sample_start: int32 [32, 7], P(('slab', 'det')), may hold values from 0 to 3840
Outputs:
- image: float32 [128, 16384], P(None, ('slab', 'det'))
Inputs may be any that keep to these rules, and one draw needn't show every extreme that they name: For detector d with home slab g = d // 4: max(0, g - 3) <= slab_range[d, 0] <= g <= slab_range[d, 1] <= min(7, g + 3); some detectors reach the full 3 on both sides where the grid allows.
All inputs are finite; a program needn't handle non-finite values.
Results may differ from a plain program's by a relative error of at most 0.007.
Values may be sent and summed in bfloat16 or wider, within the bound.
No kernel may reach another device: no remote copies, remote signals or barrier semaphores. Data moves between devices by JAX's collectives and lax.ppermute only.
A program may use at most 64 MiB of HBM per device.

v0:
```python
import jax
import jax.numpy as jnp
from jax import lax
from jax.sharding import PartitionSpec as P

KWIN = 256
NTAB = 4
RANGE = 3


def shifted(x, axis, by):
    peers = lax.axis_size(axis)
    pairs = [(i, i + by) for i in range(peers) if 0 <= i + by < peers]
    return lax.ppermute(x, axis, pairs)


def cut_windows(trace_rows, starts):

    def single(trace_row, first_index):
        return lax.dynamic_slice_in_dim(trace_row, first_index, KWIN, 1)

    return jax.vmap(single)(trace_rows, starts)


def bin_windows(windows, slot_ids, active):
    onehot = (slot_ids[:, None] == jnp.arange(NTAB, dtype=jnp.int32)[None, :]) & active[:, None]
    onehot = onehot.astype(jnp.bfloat16)
    return jnp.einsum("it,ifk->tfk", onehot, windows, preferred_element_type=jnp.float32)


def body(traces, tables, slab_range, table_slot, sample_start):
    position = lax.axis_index("slab")
    samples = traces.astype(jnp.bfloat16)
    own_active = (slab_range[:, 0] <= position) & (position <= slab_range[:, 1])
    stacked = bin_windows(
        cut_windows(samples, sample_start[:, RANGE]), table_slot[:, RANGE], own_active
    )
    for offset in list(range(-RANGE, 0)) + list(range(1, RANGE + 1)):
        target = position + offset
        active = (slab_range[:, 0] <= target) & (target <= slab_range[:, 1])
        windows = cut_windows(samples, sample_start[:, offset + RANGE])
        windows = windows * active[:, None, None].astype(jnp.bfloat16)
        arrived_windows, arrived_slots = shifted(
            (windows, table_slot[:, offset + RANGE]), "slab", offset
        )
        everything = jnp.ones(arrived_slots.shape, jnp.bool_)
        stacked = stacked + bin_windows(arrived_windows, arrived_slots, everything)
    binned = stacked.astype(jnp.bfloat16)
    partial_image = jnp.einsum(
        "tfk,tkv->fv",
        binned,
        lax.all_gather(tables, "det", axis=2, tiled=True),
        preferred_element_type=jnp.float32,
    )
    return lax.psum_scatter(partial_image, "det", scatter_dimension=1, tiled=True)


def solution(mesh):
    placed = (
        P(("slab", "det"), None, None),
        P("slab", None, "det"),
        P(("slab", "det"), None),
        P(("slab", "det"), None),
        P(("slab", "det"), None),
    )
    return jax.shard_map(
        body, mesh=mesh, in_specs=placed, out_specs=P(None, ("slab", "det")), check_vma=False
    )
```

profile of v0, /device:TPU:0, one launch (start us, length us, event | category | flops | bytes accessed | tf_op | source)
XLA Modules:
  0.0 129.3 jit_solution(1520195266104620349)
XLA Ops:
  6.5 0.0 all-gather.2.cloned.1.call-start
  6.5 0.7 all-gather.2.cloned.1.call-update
  7.3 0.0 reduce-scatter.2.cloned.1.call-start
  7.3 1.6 %fusion.21 = (s32[1,1]{1,0:T(1,128)}, s32[1,1]{1,0:T(1,128)}, s32[1,1]{1,0:T(1,128)}, s32[1,1]{1,0:T(1,128)}, s32[1,1]{1,0:T(1,128)}, /*index=5*/s32[1,1]{1,0:T(1,128)}, s32[1,1]{1,0:T(1,128)}) fusion(s32[1,7]{1,0:T(1,128)} %param.8), kind=kLoop, calls=%fused_computation.43 | loop fusion | bytes 56 | tf_op jit(solution)/shard_map/slice | solution.py:36
  8.9 3.0 %collective-permute-start.6 = (s32[1]{0:T(128)}, s32[1]{0:T(128)}, u32[]{:S(2)}, u32[]{:S(2)}) collective-permute-start(s32[1]{0:T(128)} %bitcast.33), channel_id=1, source_target_pairs={{0,4},{4,8},{8,12},{12,16},{16,20},{20,24},{24,28},{1,5},{5,9},{9,... | collective-permute-start | bytes 20 | tf_op jit(solution)/shard_map/ppermute | solution.py:14
  11.9 1.3 collective-permute-start.4
  13.1 1.3 collective-permute-start.2
  14.4 1.3 collective-permute-start
  15.7 7.7 %collective-permute-start.10 = (s32[1]{0:T(128)}, s32[1]{0:T(128)}, u32[]{:S(2)}, u32[]{:S(2)}) collective-permute-start(s32[1]{0:T(128)} %bitcast.49), channel_id=1, source_target_pairs={{0,12},{4,16},{8,20},{12,24},{16,28},{1,13},{5,17},{9,21},{13,25},... | collective-permute-start | bytes 20 | tf_op jit(solution)/shard_map/ppermute | solution.py:14
  23.4 1.3 %fusion.23 = (s32[1,1]{1,0:T(1,128)}, s32[1,1]{1,0:T(1,128)}) fusion(s32[1,2]{1,0:T(1,128)} %param.7), kind=kLoop, calls=%fused_computation.45 | loop fusion | bytes 16 | tf_op jit(solution)/shard_map/slice | solution.py:34
  33.7 1.6 %fusion.22 = (s32[1,1]{1,0:T(1,128)}, s32[1,1]{1,0:T(1,128)}, s32[1,1]{1,0:T(1,128)}, s32[1,1]{1,0:T(1,128)}, s32[1,1]{1,0:T(1,128)}, /*index=5*/s32[1,1]{1,0:T(1,128)}, s32[1,1]{1,0:T(1,128)}) fusion(s32[1,7]{1,0:T(1,128)} %param.9), kind=kLoop, calls=%fused_computation.44 | loop fusion | bytes 56 | tf_op jit(solution)/shard_map/slice | solution.py:36
  44.2 1.7 %convert_element_type.10 = bf16[1,128,4096]{2,1,0:T(8,128)(2,1)S(1)} convert(f32[1,128,4096]{2,1,0:T(8,128)} %param.5) | non-fusion elementwise | flops 524288 | bytes 3145728 | tf_op jit(solution)/shard_map/convert_element_type | solution.py:33
  50.4 0.6 fusion.14
  51.0 0.2 bitcast_convert_fusion.6
  51.2 0.0 collective-permute-done.6
  51.2 5.9 %collective-permute-start.8 = (s32[1]{0:T(128)}, s32[1]{0:T(128)}, u32[]{:S(2)}, u32[]{:S(2)}) collective-permute-start(s32[1]{0:T(128)} %bitcast.41), channel_id=1, source_target_pairs={{0,8},{4,12},{8,16},{12,20},{16,24},{20,28},{1,9},{5,13},{9,17},{1... | collective-permute-start | bytes 20 | tf_op jit(solution)/shard_map/ppermute | solution.py:14
  57.1 0.7 fusion.18
  57.8 0.0 collective-permute-done.4
  57.8 1.3 %collective-permute-start.11 = (bf16[1,128,256]{2,1,0:T(8,128)(2,1)S(1)}, bf16[1,128,256]{2,1,0:T(8,128)(2,1)S(1)}, u32[]{:S(2)}, u32[]{:S(2)}) collective-permute-start(bf16[1,128,256]{2,1,0:T(8,128)(2,1)S(1)} %get-tuple-element.83), channel_id=1, source_target_pairs={{0,12},{4,16},{8,20},{12,24},{16,28},{1,13},{5,17},{9,21},{13,25},... | collective-permute-start | bytes 196616 | tf_op jit(solution)/shard_map/ppermute | solution.py:14
  59.1 0.6 fusion.17
  59.8 0.0 collective-permute-done.2
  59.8 2.9 %collective-permute-start.9 = (bf16[1,128,256]{2,1,0:T(8,128)(2,1)S(1)}, bf16[1,128,256]{2,1,0:T(8,128)(2,1)S(1)}, u32[]{:S(2)}, u32[]{:S(2)}) collective-permute-start(bf16[1,128,256]{2,1,0:T(8,128)(2,1)S(1)} %get-tuple-element.84), channel_id=1, source_target_pairs={{0,8},{4,12},{8,16},{12,20},{16,24},{20,28},{1,9},{5,13},{9,17},{1... | collective-permute-start | bytes 196616 | tf_op jit(solution)/shard_map/ppermute | solution.py:14
  62.6 0.6 fusion.16
  63.3 0.0 collective-permute-done
  63.3 1.3 %collective-permute-start.7 = (bf16[1,128,256]{2,1,0:T(8,128)(2,1)S(1)}, bf16[1,128,256]{2,1,0:T(8,128)(2,1)S(1)}, u32[]{:S(2)}, u32[]{:S(2)}) collective-permute-start(bf16[1,128,256]{2,1,0:T(8,128)(2,1)S(1)} %get-tuple-element.85), channel_id=1, source_target_pairs={{0,4},{4,8},{8,12},{12,16},{16,20},{20,24},{24,28},{1,5},{5,9},{9,... | collective-permute-start | bytes 196616 | tf_op jit(solution)/shard_map/ppermute | solution.py:14
  64.6 0.6 fusion.15
  65.2 0.0 collective-permute-done.10
  65.3 1.3 collective-permute-start.5
  66.6 0.6 fusion.20
  67.2 0.0 collective-permute-done.8
  67.2 1.3 collective-permute-start.3
  68.5 0.7 fusion.19
  69.2 0.0 collective-permute-done.11
  69.2 1.3 collective-permute-start.1
  70.5 0.0 collective-permute-done.9
  70.5 0.0 collective-permute-done.7
  70.6 0.0 collective-permute-done.5
  70.6 4.5 %collective-permute-done.3 = bf16[1,128,256]{2,1,0:T(8,128)(2,1)S(1)} collective-permute-done((bf16[1,128,256]{2,1,0:T(8,128)(2,1)S(1)}, bf16[1,128,256]{2,1,0:T(8,128)(2,1)S(1)}, u32[]{:S(2)}, u32[]{:S(2)}) %collective-permute-start.3) | collective-permute-done | bytes 65568 | tf_op jit(solution)/shard_map/ppermute | solution.py:14
  75.1 1.9 %collective-permute-done.1 = bf16[1,128,256]{2,1,0:T(8,128)(2,1)S(1)} collective-permute-done((bf16[1,128,256]{2,1,0:T(8,128)(2,1)S(1)}, bf16[1,128,256]{2,1,0:T(8,128)(2,1)S(1)}, u32[]{:S(2)}, u32[]{:S(2)}) %collective-permute-start.1) | collective-permute-done | bytes 65568 | tf_op jit(solution)/shard_map/ppermute | solution.py:14
  77.0 15.4 %all-gather.2.cloned.1.call-done = bf16[4,256,2048]{2,1,0:T(8,128)(2,1)} async-done(((bf16[4,256,512]{2,1,0:T(8,128)(2,1)}), bf16[4,256,2048]{2,1,0:T(8,128)(2,1)}) %all-gather.2.cloned.1.call-update) | async-done | bytes 4194320 | tf_op jit(solution)/shard_map/all_gather | solution.py:52
  92.4 4.1 %convolution_bitcast_fusion = f32[128,2048]{1,0:T(8,128)} fusion(bf16[4,256,2048]{2,1,0:T(8,128)(2,1)} %all-gather.2.cloned.1.call-done, f32[128,256]{1,0:T(8,128)S(1)} %bitcast_convert_fusion, f32[4]{0:T(128)S(1)} %fusion.20, f32[128,256]{1,0:T(8,128)S(1)} %bitcast_convert_fusion.1, f32[4]{0:T(128)S(1)} %fusion.19, f32[128,256]{1,0:T(8,128)S(1)} %bitcast_convert_fusion.2, ...), kind=kOutput, calls=%fused_computation | convolution fusion | flops 538705920 | bytes 6160496 | tf_op jit(solution)/shard_map/tfk,tkv->fv/dot_general | solution.py:49
  96.5 0.0 reduce-scatter.2.cloned.1.call-update
  96.5 25.9 %reduce-scatter.2.cloned.1.call-done = f32[128,512]{1,0:T(8,128)} async-done(((f32[128,2048]{1,0:T(8,128)}), f32[128,512]{1,0:T(8,128)}) %reduce-scatter.2.cloned.1.call-update) | async-done | bytes 262160 | tf_op jit(solution)/shard_map/reduce_scatter | solution.py:55
  (6 shorter events, 0.1 us)
Async XLA Ops:
  6.5 85.9 %all-gather.2.cloned.1.call-start = ((), (), s32[]{:S(2)}) async-start(), calls=%async_computation.1 | async-start | bytes 5242880 | tf_op jit(solution)/shard_map/all_gather | solution.py:52
  7.3 115.2 %reduce-scatter.2.cloned.1.call-start = ((), (), s32[]{:S(2)}) async-start(), calls=%async_computation.2 | async-start | bytes 1310720 | tf_op jit(solution)/shard_map/reduce_scatter | solution.py:55
  8.9 42.3 %collective-permute-start.6 = (s32[1]{0:T(128)}, s32[1]{0:T(128)}, u32[]{:S(2)}, u32[]{:S(2)}) collective-permute-start(s32[1]{0:T(128)} %bitcast.33), channel_id=1, source_target_pairs={{0,4},{4,8},{8,12},{12,16},{16,20},{20,24},{24,28},{1,5},{5,9},{9,... | collective-permute-start | bytes 20 | tf_op jit(solution)/shard_map/ppermute | solution.py:14
  11.9 46.0 %collective-permute-start.4 = (s32[1]{0:T(128)}, s32[1]{0:T(128)}, u32[]{:S(2)}, u32[]{:S(2)}) collective-permute-start(s32[1]{0:T(128)} %bitcast.25), channel_id=1, source_target_pairs={{4,0},{8,4},{12,8},{16,12},{20,16},{24,20},{28,24},{5,1},{9,5},{13... | collective-permute-start | bytes 20 | tf_op jit(solution)/shard_map/ppermute | solution.py:14
  13.1 46.6 %collective-permute-start.2 = (s32[1]{0:T(128)}, s32[1]{0:T(128)}, u32[]{:S(2)}, u32[]{:S(2)}) collective-permute-start(s32[1]{0:T(128)} %bitcast.17), channel_id=1, source_target_pairs={{8,0},{12,4},{16,8},{20,12},{24,16},{28,20},{9,1},{13,5},{17,9},{2... | collective-permute-start | bytes 20 | tf_op jit(solution)/shard_map/ppermute | solution.py:14
  14.4 48.8 %collective-permute-start = (s32[1]{0:T(128)}, s32[1]{0:T(128)}, u32[]{:S(2)}, u32[]{:S(2)}) collective-permute-start(s32[1]{0:T(128)} %bitcast.9), channel_id=1, source_target_pairs={{12,0},{16,4},{20,8},{24,12},{28,16},{13,1},{17,5},{21,9},{25,13},... | collective-permute-start | bytes 20 | tf_op jit(solution)/shard_map/ppermute | solution.py:14
  15.7 49.5 %collective-permute-start.10 = (s32[1]{0:T(128)}, s32[1]{0:T(128)}, u32[]{:S(2)}, u32[]{:S(2)}) collective-permute-start(s32[1]{0:T(128)} %bitcast.49), channel_id=1, source_target_pairs={{0,12},{4,16},{8,20},{12,24},{16,28},{1,13},{5,17},{9,21},{13,25},... | collective-permute-start | bytes 20 | tf_op jit(solution)/shard_map/ppermute | solution.py:14
  51.2 16.0 %collective-permute-start.8 = (s32[1]{0:T(128)}, s32[1]{0:T(128)}, u32[]{:S(2)}, u32[]{:S(2)}) collective-permute-start(s32[1]{0:T(128)} %bitcast.41), channel_id=1, source_target_pairs={{0,8},{4,12},{8,16},{12,20},{16,24},{20,28},{1,9},{5,13},{9,17},{1... | collective-permute-start | bytes 20 | tf_op jit(solution)/shard_map/ppermute | solution.py:14
  57.8 11.4 %collective-permute-start.11 = (bf16[1,128,256]{2,1,0:T(8,128)(2,1)S(1)}, bf16[1,128,256]{2,1,0:T(8,128)(2,1)S(1)}, u32[]{:S(2)}, u32[]{:S(2)}) collective-permute-start(bf16[1,128,256]{2,1,0:T(8,128)(2,1)S(1)} %get-tuple-element.83), channel_id=1, source_target_pairs={{0,12},{4,16},{8,20},{12,24},{16,28},{1,13},{5,17},{9,21},{13,25},... | collective-permute-start | bytes 196616 | tf_op jit(solution)/shard_map/ppermute | solution.py:14
  59.8 10.7 %collective-permute-start.9 = (bf16[1,128,256]{2,1,0:T(8,128)(2,1)S(1)}, bf16[1,128,256]{2,1,0:T(8,128)(2,1)S(1)}, u32[]{:S(2)}, u32[]{:S(2)}) collective-permute-start(bf16[1,128,256]{2,1,0:T(8,128)(2,1)S(1)} %get-tuple-element.84), channel_id=1, source_target_pairs={{0,8},{4,12},{8,16},{12,20},{16,24},{20,28},{1,9},{5,13},{9,17},{1... | collective-permute-start | bytes 196616 | tf_op jit(solution)/shard_map/ppermute | solution.py:14
  63.3 7.2 %collective-permute-start.7 = (bf16[1,128,256]{2,1,0:T(8,128)(2,1)S(1)}, bf16[1,128,256]{2,1,0:T(8,128)(2,1)S(1)}, u32[]{:S(2)}, u32[]{:S(2)}) collective-permute-start(bf16[1,128,256]{2,1,0:T(8,128)(2,1)S(1)} %get-tuple-element.85), channel_id=1, source_target_pairs={{0,4},{4,8},{8,12},{12,16},{16,20},{20,24},{24,28},{1,5},{5,9},{9,... | collective-permute-start | bytes 196616 | tf_op jit(solution)/shard_map/ppermute | solution.py:14
  65.3 5.3 %collective-permute-start.5 = (bf16[1,128,256]{2,1,0:T(8,128)(2,1)S(1)}, bf16[1,128,256]{2,1,0:T(8,128)(2,1)S(1)}, u32[]{:S(2)}, u32[]{:S(2)}) collective-permute-start(bf16[1,128,256]{2,1,0:T(8,128)(2,1)S(1)} %get-tuple-element.86), channel_id=1, source_target_pairs={{4,0},{8,4},{12,8},{16,12},{20,16},{24,20},{28,24},{5,1},{9,5},{13... | collective-permute-start | bytes 196616 | tf_op jit(solution)/shard_map/ppermute | solution.py:14
  67.2 7.9 %collective-permute-start.3 = (bf16[1,128,256]{2,1,0:T(8,128)(2,1)S(1)}, bf16[1,128,256]{2,1,0:T(8,128)(2,1)S(1)}, u32[]{:S(2)}, u32[]{:S(2)}) collective-permute-start(bf16[1,128,256]{2,1,0:T(8,128)(2,1)S(1)} %get-tuple-element.87), channel_id=1, source_target_pairs={{8,0},{12,4},{16,8},{20,12},{24,16},{28,20},{9,1},{13,5},{17,9},{2... | collective-permute-start | bytes 196616 | tf_op jit(solution)/shard_map/ppermute | solution.py:14
  69.2 7.8 %collective-permute-start.1 = (bf16[1,128,256]{2,1,0:T(8,128)(2,1)S(1)}, bf16[1,128,256]{2,1,0:T(8,128)(2,1)S(1)}, u32[]{:S(2)}, u32[]{:S(2)}) collective-permute-start(bf16[1,128,256]{2,1,0:T(8,128)(2,1)S(1)} %get-tuple-element.88), channel_id=1, source_target_pairs={{12,0},{16,4},{20,8},{24,12},{28,16},{13,1},{17,5},{21,9},{25,13},... | collective-permute-start | bytes 196616 | tf_op jit(solution)/shard_map/ppermute | solution.py:14
Sparse Core Ops, SparseCore 0:
  8.9 83.4 all-gather.1
  96.6 25.7 reduce-scatter.1
where the time goes:
time: 130 us; the launch traced here: 129 us
  waiting for transfers between devices  48.5 us (37%)
  between operations  36 us (28%)
  starting transfers between devices  29.8 us (23%)
  other arithmetic  6.48 us (5%)
  local copies, waits for them, and re-layouts  4.5 us (3%)
  matrix products  4.07 us (3%)
    ppermute x12, starting transfers between devices, shifted(): return lax.ppermute(x, axis, pairs)  29.8 us
    reduce_scatter x1, waiting for transfers between devices, body(): lax.psum_scatter(partial_image, 'det', scatter_dimension=1, tiled=True)  25.9 us
    all_gather x1, waiting for transfers between devices, body(): lax.all_gather(tables, 'det', axis=2, tiled=True)  15.4 us
    ppermute x12, waiting for transfers between devices, shifted(): return lax.ppermute(x, axis, pairs)  6.42 us
    another operation x14, other arithmetic  4.75 us
    dot_general x1, matrix products, body(): jnp.einsum('tfk,tkv->fv', binned, lax.all_gather(tables, 'det', axis=2, t...  4.07 us
  transfers between devices with their start and end apart: 14, of which 4 were waited for; matrix products, arithmetic and copies ran while one was open for 8% of the time, Pallas kernels for 0%

commit v1 on v0

--- a/solution.py
+++ b/solution.py
@@ -6,6 +6,20 @@
 KWIN = 256
 NTAB = 4
 RANGE = 3
+
+
+def ring_apply(x, axis, dim, make, out_dim):
+    ways, here, step = (lax.axis_size(axis), lax.axis_index(axis), x.shape[dim])
+    earlier, later = ([], [])
+    going_up = going_down = x
+    for far in range(ways // 2 + 1):
+        earlier.append(make(going_up, (here - far) % ways * step))
+        if 0 < far < ways - ways // 2:
+            later.append(make(going_down, (here + far) % ways * step))
+        going_up = lax.ppermute(going_up, axis, [(d, (d + 1) % ways) for d in range(ways)])
+        going_down = lax.ppermute(going_down, axis, [(d, (d - 1) % ways) for d in range(ways)])
+    line = jnp.concatenate([*earlier[::-1], *later], axis=out_dim)
+    return jnp.roll(line, (here - ways // 2) * earlier[0].shape[out_dim], axis=out_dim)
 
 
 def shifted(x, axis, by):
@@ -46,11 +60,14 @@
         everything = jnp.ones(arrived_slots.shape, jnp.bool_)
         stacked = stacked + bin_windows(arrived_windows, arrived_slots, everything)
     binned = stacked.astype(jnp.bfloat16)
-    partial_image = jnp.einsum(
-        "tfk,tkv->fv",
-        binned,
-        lax.all_gather(tables, "det", axis=2, tiled=True),
-        preferred_element_type=jnp.float32,
+    partial_image = ring_apply(
+        tables,
+        "det",
+        2,
+        lambda part, start: jnp.einsum(
+            "tfk,tkv->fv", binned, part, preferred_element_type=jnp.float32
+        ),
+        1,
     )
     return lax.psum_scatter(partial_image, "det", scatter_dimension=1, tiled=True)
 

time: 130 us -> 151 us (1.16)
  waiting for transfers between devices: 48.5 us -> 65.2 us
  starting transfers between devices: 29.8 us -> 36.2 us
  matrix products: 4.07 us -> 1.24 us
    ppermute x0 -> x3, waiting for transfers between devices: none -> 20.5 us  [the longest x2 20.5 us: ring_apply(): lax.ppermute(going_up, axis, [(d, (d + 1) % ways) for d in range(ways)])]
    all_gather x1 -> x0, waiting for transfers between devices: 15.4 us -> none  [body(): lax.all_gather(tables, 'det', axis=2, tiled=True)]
    ppermute x12, waiting for transfers between devices: 6.42 us -> 14.3 us  [shifted(): return lax.ppermute(x, axis, pairs)]
    ppermute x0 -> x3, starting transfers between devices: none -> 5.14 us  [the longest x2 3.11 us: ring_apply(): lax.ppermute(going_up, axis, [(d, (d + 1) % ways) for d in range(ways)])]
    reduce_scatter x1, waiting for transfers between devices: 25.9 us -> 30.4 us  [body(): lax.psum_scatter(partial_image, 'det', scatter_dimension=1, tiled=True)]
    dot_general x1 -> x4, matrix products: 4.07 us -> 1.24 us  [body(): jnp.einsum('tfk,tkv->fv', binned, part, preferred_element_type=jnp.float32)]
  transfers between devices with their start and end apart: 14 -> 16, of which waited for: 4 -> 9; matrix products, arithmetic and copies ran while one was open for 8% -> 8% of each run, Pallas kernels for 0% -> 0%
where the time goes in v1:
time: 151 us; the launch traced here: 150 us
  waiting for transfers between devices  65.2 us (43%)
  starting transfers between devices  36.2 us (24%)
  between operations  36.1 us (24%)
  other arithmetic  6.75 us (4%)
  local copies, waits for them, and re-layouts  4.79 us (3%)
    ppermute x12, starting transfers between devices, shifted(): return lax.ppermute(x, axis, pairs)  31 us
    reduce_scatter x1, waiting for transfers between devices, body(): lax.psum_scatter(partial_image, 'det', scatter_dimension=1, tiled=True)  30.4 us
    ppermute x2, waiting for transfers between devices, ring_apply(): lax.ppermute(going_up, axis, [(d, (d + 1) % ways) for d in range(ways)])  20.5 us
    ppermute x12, waiting for transfers between devices, shifted(): return lax.ppermute(x, axis, pairs)  14.3 us
    another operation x14, other arithmetic  4.73 us
    ppermute x2, starting transfers between devices, ring_apply(): lax.ppermute(going_up, axis, [(d, (d + 1) % ways) for d in range(ways)])  3.11 us
  transfers between devices with their start and end apart: 16, of which 9 were waited for; matrix products, arithmetic and copies ran while one was open for 8% of the time, Pallas kernels for 0%

profile of v1, /device:TPU:0, one launch (start us, length us, event | category | flops | bytes accessed | tf_op | source)
XLA Modules:
  0.0 150.2 jit_solution(13815892210423949015)
XLA Ops:
  6.5 0.0 reduce-scatter.2.cloned.1.call-start
  6.5 3.1 %collective-permute-start.12 = (bf16[4,256,512]{2,1,0:T(8,128)(2,1)}, bf16[4,256,512]{2,1,0:T(8,128)(2,1)S(1)}, u32[]{:S(2)}, u32[]{:S(2)}) collective-permute-start(bf16[4,256,512]{2,1,0:T(8,128)(2,1)} %param.6), channel_id=1, source_target_pairs={{0,1},{1,2},{2,3},{3,0},{4,5},{5,6},{6,7},{7,4},{8,9},{9,10},{10,1... | collective-permute-start | bytes 3145736 | tf_op jit(solution)/shard_map/ppermute | solution.py:19
  9.6 2.0 %collective-permute-start.14 = (bf16[4,256,512]{2,1,0:T(8,128)(2,1)}, bf16[4,256,512]{2,1,0:T(8,128)(2,1)S(1)}, u32[]{:S(2)}, u32[]{:S(2)}) collective-permute-start(bf16[4,256,512]{2,1,0:T(8,128)(2,1)} %param.6), channel_id=1, source_target_pairs={{0,3},{1,0},{2,1},{3,2},{4,7},{5,4},{6,5},{7,6},{8,11},{9,8},{10,9... | collective-permute-start | bytes 3145736 | tf_op jit(solution)/shard_map/ppermute | solution.py:20
  11.6 1.3 fusion.9
  20.4 1.6 %fusion.8 = (s32[1,1]{1,0:T(1,128)}, s32[1,1]{1,0:T(1,128)}, s32[1,1]{1,0:T(1,128)}, s32[1,1]{1,0:T(1,128)}, s32[1,1]{1,0:T(1,128)}, /*index=5*/s32[1,1]{1,0:T(1,128)}, s32[1,1]{1,0:T(1,128)}) fusion(s32[1,7]{1,0:T(1,128)} %param.9), kind=kLoop, calls=%fused_computation.42 | loop fusion | bytes 56 | tf_op jit(solution)/shard_map/slice | solution.py:50
  31.0 0.0 copy-start.1
  31.1 1.7 %convert_element_type.10 = bf16[1,128,4096]{2,1,0:T(8,128)(2,1)S(1)} convert(f32[1,128,4096]{2,1,0:T(8,128)} %param.5) | non-fusion elementwise | flops 524288 | bytes 3145728 | tf_op jit(solution)/shard_map/convert_element_type | solution.py:47
  37.3 0.2 bitcast_convert_fusion.6
  37.5 2.6 %collective-permute-start.11 = (bf16[1,128,256]{2,1,0:T(8,128)(2,1)S(1)}, bf16[1,128,256]{2,1,0:T(8,128)(2,1)S(1)}, u32[]{:S(2)}, u32[]{:S(2)}) collective-permute-start(bf16[1,128,256]{2,1,0:T(8,128)(2,1)S(1)} %get-tuple-element.83), channel_id=1, source_target_pairs={{0,12},{4,16},{8,20},{12,24},{16,28},{1,13},{5,17},{9,21},{13,25},... | collective-permute-start | bytes 196616 | tf_op jit(solution)/shard_map/ppermute | solution.py:28
  40.1 3.4 %collective-permute-start.9 = (bf16[1,128,256]{2,1,0:T(8,128)(2,1)S(1)}, bf16[1,128,256]{2,1,0:T(8,128)(2,1)S(1)}, u32[]{:S(2)}, u32[]{:S(2)}) collective-permute-start(bf16[1,128,256]{2,1,0:T(8,128)(2,1)S(1)} %get-tuple-element.84), channel_id=1, source_target_pairs={{0,8},{4,12},{8,16},{12,20},{16,24},{20,28},{1,9},{5,13},{9,17},{1... | collective-permute-start | bytes 196616 | tf_op jit(solution)/shard_map/ppermute | solution.py:28
  43.5 0.0 copy-done.1
  43.5 0.7 fusion.7
  44.2 1.3 collective-permute-start
  46.8 0.7 fusion
  47.4 1.8 %collective-permute-done = s32[1]{0:T(128)} collective-permute-done((s32[1]{0:T(128)}, s32[1]{0:T(128)}, u32[]{:S(2)}, u32[]{:S(2)}) %collective-permute-start) | collective-permute-done | bytes 36 | tf_op jit(solution)/shard_map/ppermute | solution.py:28
  49.3 1.3 collective-permute-start.2
  50.5 0.6 fusion.1
  51.2 4.1 %collective-permute-done.2 = s32[1]{0:T(128)} collective-permute-done((s32[1]{0:T(128)}, s32[1]{0:T(128)}, u32[]{:S(2)}, u32[]{:S(2)}) %collective-permute-start.2) | collective-permute-done | bytes 36 | tf_op jit(solution)/shard_map/ppermute | solution.py:28
  55.2 1.3 collective-permute-start.4
  56.5 0.6 fusion.2
  57.2 1.1 collective-permute-done.4
  58.3 5.7 %collective-permute-start.6 = (s32[1]{0:T(128)}, s32[1]{0:T(128)}, u32[]{:S(2)}, u32[]{:S(2)}) collective-permute-start(s32[1]{0:T(128)} %bitcast.33), channel_id=1, source_target_pairs={{0,4},{4,8},{8,12},{12,16},{16,20},{20,24},{24,28},{1,5},{5,9},{9,... | collective-permute-start | bytes 20 | tf_op jit(solution)/shard_map/ppermute | solution.py:28
  64.0 0.7 fusion.3
  64.7 0.0 collective-permute-done.6
  64.7 4.5 %collective-permute-start.8 = (s32[1]{0:T(128)}, s32[1]{0:T(128)}, u32[]{:S(2)}, u32[]{:S(2)}) collective-permute-start(s32[1]{0:T(128)} %bitcast.41), channel_id=1, source_target_pairs={{0,8},{4,12},{8,16},{12,20},{16,24},{20,28},{1,9},{5,13},{9,17},{1... | collective-permute-start | bytes 20 | tf_op jit(solution)/shard_map/ppermute | solution.py:28
  69.2 0.6 fusion.4
  69.7 0.3 collective-permute-done.8
  70.1 1.8 %collective-permute-start.10 = (s32[1]{0:T(128)}, s32[1]{0:T(128)}, u32[]{:S(2)}, u32[]{:S(2)}) collective-permute-start(s32[1]{0:T(128)} %bitcast.49), channel_id=1, source_target_pairs={{0,12},{4,16},{8,20},{12,24},{16,28},{1,13},{5,17},{9,21},{13,25},... | collective-permute-start | bytes 20 | tf_op jit(solution)/shard_map/ppermute | solution.py:28
  71.9 0.7 fusion.5
  72.5 0.1 collective-permute-done.10
  72.7 5.5 %collective-permute-start.7 = (bf16[1,128,256]{2,1,0:T(8,128)(2,1)S(1)}, bf16[1,128,256]{2,1,0:T(8,128)(2,1)S(1)}, u32[]{:S(2)}, u32[]{:S(2)}) collective-permute-start(bf16[1,128,256]{2,1,0:T(8,128)(2,1)S(1)} %get-tuple-element.85), channel_id=1, source_target_pairs={{0,4},{4,8},{8,12},{12,16},{16,20},{20,24},{24,28},{1,5},{5,9},{9,... | collective-permute-start | bytes 196616 | tf_op jit(solution)/shard_map/ppermute | solution.py:28
  78.2 0.6 fusion.6
  78.7 0.0 collective-permute-done.11
  78.7 1.3 collective-permute-start.5
  80.1 0.0 collective-permute-done.9
  80.1 1.3 collective-permute-start.3
  81.4 0.0 collective-permute-done.7
  81.4 1.3 collective-permute-start.1
  82.7 0.0 collective-permute-done.12
  82.7 0.1 collective-permute-start.13
  82.8 0.0 collective-permute-done.5
  82.8 3.6 %collective-permute-done.3 = bf16[1,128,256]{2,1,0:T(8,128)(2,1)S(1)} collective-permute-done((bf16[1,128,256]{2,1,0:T(8,128)(2,1)S(1)}, bf16[1,128,256]{2,1,0:T(8,128)(2,1)S(1)}, u32[]{:S(2)}, u32[]{:S(2)}) %collective-permute-start.3) | collective-permute-done | bytes 65568 | tf_op jit(solution)/shard_map/ppermute | solution.py:28
  86.5 3.2 %collective-permute-done.1 = bf16[1,128,256]{2,1,0:T(8,128)(2,1)S(1)} collective-permute-done((bf16[1,128,256]{2,1,0:T(8,128)(2,1)S(1)}, bf16[1,128,256]{2,1,0:T(8,128)(2,1)S(1)}, u32[]{:S(2)}, u32[]{:S(2)}) %collective-permute-start.1) | collective-permute-done | bytes 65568 | tf_op jit(solution)/shard_map/ppermute | solution.py:28
  89.7 0.3 add_convert_fusion
  90.0 0.0 copy-start
  90.0 20.5 %collective-permute-done.13 = bf16[4,256,512]{2,1,0:T(8,128)(2,1)S(1)} collective-permute-done((bf16[4,256,512]{2,1,0:T(8,128)(2,1)S(1)}, bf16[4,256,512]{2,1,0:T(8,128)(2,1)S(1)}, u32[]{:S(2)}, u32[]{:S(2)}) %collective-permute-start.13) | collective-permute-done | bytes 1048608 | tf_op jit(solution)/shard_map/ppermute | solution.py:19
  110.4 0.3 constant_dynamic-update-slice_fusion.7
  110.8 0.3 constant_dynamic-update-slice_fusion.6
  111.1 0.0 copy-done
  111.1 0.3 constant_dynamic-update-slice_fusion.5
  111.4 0.0 collective-permute-done.14
  111.4 0.3 constant_dynamic-update-slice_fusion.4
  111.8 1.1 constant_dynamic-slice_fusion
  112.9 0.0 reduce-scatter.2.cloned.1.call-update
  113.0 30.4 %reduce-scatter.2.cloned.1.call-done = f32[128,512]{1,0:T(8,128)} async-done(((f32[128,2048]{1,0:T(8,128)}), f32[128,512]{1,0:T(8,128)}) %reduce-scatter.2.cloned.1.call-update) | async-done | bytes 262160 | tf_op jit(solution)/shard_map/reduce_scatter | solution.py:72
  (10 shorter events, 0.1 us)
Async XLA Ops:
  6.5 136.8 %reduce-scatter.2.cloned.1.call-start = ((), (), s32[]{:S(2)}) async-start(), calls=%async_computation.1 | async-start | bytes 1310720 | tf_op jit(solution)/shard_map/reduce_scatter | solution.py:72
  6.5 76.2 %collective-permute-start.12 = (bf16[4,256,512]{2,1,0:T(8,128)(2,1)}, bf16[4,256,512]{2,1,0:T(8,128)(2,1)S(1)}, u32[]{:S(2)}, u32[]{:S(2)}) collective-permute-start(bf16[4,256,512]{2,1,0:T(8,128)(2,1)} %param.6), channel_id=1, source_target_pairs={{0,1},{1,2},{2,3},{3,0},{4,5},{5,6},{6,7},{7,4},{8,9},{9,10},{10,1... | collective-permute-start | bytes 3145736 | tf_op jit(solution)/shard_map/ppermute | solution.py:19
  9.6 101.8 %collective-permute-start.14 = (bf16[4,256,512]{2,1,0:T(8,128)(2,1)}, bf16[4,256,512]{2,1,0:T(8,128)(2,1)S(1)}, u32[]{:S(2)}, u32[]{:S(2)}) collective-permute-start(bf16[4,256,512]{2,1,0:T(8,128)(2,1)} %param.6), channel_id=1, source_target_pairs={{0,3},{1,0},{2,1},{3,2},{4,7},{5,4},{6,5},{7,6},{8,11},{9,8},{10,9... | collective-permute-start | bytes 3145736 | tf_op jit(solution)/shard_map/ppermute | solution.py:20
  31.0 12.5 %copy-start.1 = (s32[1,7]{1,0:T(1,128)S(1)}, s32[1,7]{1,0:T(1,128)}, u32[]{:S(2)}) copy-start(s32[1,7]{1,0:T(1,128)} %param.8) | copy-start | bytes 88
  37.5 41.2 %collective-permute-start.11 = (bf16[1,128,256]{2,1,0:T(8,128)(2,1)S(1)}, bf16[1,128,256]{2,1,0:T(8,128)(2,1)S(1)}, u32[]{:S(2)}, u32[]{:S(2)}) collective-permute-start(bf16[1,128,256]{2,1,0:T(8,128)(2,1)S(1)} %get-tuple-element.83), channel_id=1, source_target_pairs={{0,12},{4,16},{8,20},{12,24},{16,28},{1,13},{5,17},{9,21},{13,25},... | collective-permute-start | bytes 196616 | tf_op jit(solution)/shard_map/ppermute | solution.py:28
  40.1 40.0 %collective-permute-start.9 = (bf16[1,128,256]{2,1,0:T(8,128)(2,1)S(1)}, bf16[1,128,256]{2,1,0:T(8,128)(2,1)S(1)}, u32[]{:S(2)}, u32[]{:S(2)}) collective-permute-start(bf16[1,128,256]{2,1,0:T(8,128)(2,1)S(1)} %get-tuple-element.84), channel_id=1, source_target_pairs={{0,8},{4,12},{8,16},{12,20},{16,24},{20,28},{1,9},{5,13},{9,17},{1... | collective-permute-start | bytes 196616 | tf_op jit(solution)/shard_map/ppermute | solution.py:28
  44.2 5.0 %collective-permute-start = (s32[1]{0:T(128)}, s32[1]{0:T(128)}, u32[]{:S(2)}, u32[]{:S(2)}) collective-permute-start(s32[1]{0:T(128)} %bitcast.9), channel_id=1, source_target_pairs={{12,0},{16,4},{20,8},{24,12},{28,16},{13,1},{17,5},{21,9},{25,13},... | collective-permute-start | bytes 20 | tf_op jit(solution)/shard_map/ppermute | solution.py:28
  49.3 6.0 %collective-permute-start.2 = (s32[1]{0:T(128)}, s32[1]{0:T(128)}, u32[]{:S(2)}, u32[]{:S(2)}) collective-permute-start(s32[1]{0:T(128)} %bitcast.17), channel_id=1, source_target_pairs={{8,0},{12,4},{16,8},{20,12},{24,16},{28,20},{9,1},{13,5},{17,9},{2... | collective-permute-start | bytes 20 | tf_op jit(solution)/shard_map/ppermute | solution.py:28
  55.2 3.1 %collective-permute-start.4 = (s32[1]{0:T(128)}, s32[1]{0:T(128)}, u32[]{:S(2)}, u32[]{:S(2)}) collective-permute-start(s32[1]{0:T(128)} %bitcast.25), channel_id=1, source_target_pairs={{4,0},{8,4},{12,8},{16,12},{20,16},{24,20},{28,24},{5,1},{9,5},{13... | collective-permute-start | bytes 20 | tf_op jit(solution)/shard_map/ppermute | solution.py:28
  58.3 6.4 %collective-permute-start.6 = (s32[1]{0:T(128)}, s32[1]{0:T(128)}, u32[]{:S(2)}, u32[]{:S(2)}) collective-permute-start(s32[1]{0:T(128)} %bitcast.33), channel_id=1, source_target_pairs={{0,4},{4,8},{8,12},{12,16},{16,20},{20,24},{24,28},{1,5},{5,9},{9,... | collective-permute-start | bytes 20 | tf_op jit(solution)/shard_map/ppermute | solution.py:28
  64.7 5.4 %collective-permute-start.8 = (s32[1]{0:T(128)}, s32[1]{0:T(128)}, u32[]{:S(2)}, u32[]{:S(2)}) collective-permute-start(s32[1]{0:T(128)} %bitcast.41), channel_id=1, source_target_pairs={{0,8},{4,12},{8,16},{12,20},{16,24},{20,28},{1,9},{5,13},{9,17},{1... | collective-permute-start | bytes 20 | tf_op jit(solution)/shard_map/ppermute | solution.py:28
  70.1 2.6 %collective-permute-start.10 = (s32[1]{0:T(128)}, s32[1]{0:T(128)}, u32[]{:S(2)}, u32[]{:S(2)}) collective-permute-start(s32[1]{0:T(128)} %bitcast.49), channel_id=1, source_target_pairs={{0,12},{4,16},{8,20},{12,24},{16,28},{1,13},{5,17},{9,21},{13,25},... | collective-permute-start | bytes 20 | tf_op jit(solution)/shard_map/ppermute | solution.py:28
  72.7 8.7 %collective-permute-start.7 = (bf16[1,128,256]{2,1,0:T(8,128)(2,1)S(1)}, bf16[1,128,256]{2,1,0:T(8,128)(2,1)S(1)}, u32[]{:S(2)}, u32[]{:S(2)}) collective-permute-start(bf16[1,128,256]{2,1,0:T(8,128)(2,1)S(1)} %get-tuple-element.85), channel_id=1, source_target_pairs={{0,4},{4,8},{8,12},{12,16},{16,20},{20,24},{24,28},{1,5},{5,9},{9,... | collective-permute-start | bytes 196616 | tf_op jit(solution)/shard_map/ppermute | solution.py:28
  78.7 4.1 %collective-permute-start.5 = (bf16[1,128,256]{2,1,0:T(8,128)(2,1)S(1)}, bf16[1,128,256]{2,1,0:T(8,128)(2,1)S(1)}, u32[]{:S(2)}, u32[]{:S(2)}) collective-permute-start(bf16[1,128,256]{2,1,0:T(8,128)(2,1)S(1)} %get-tuple-element.86), channel_id=1, source_target_pairs={{4,0},{8,4},{12,8},{16,12},{20,16},{24,20},{28,24},{5,1},{9,5},{13... | collective-permute-start | bytes 196616 | tf_op jit(solution)/shard_map/ppermute | solution.py:28
  80.1 6.4 %collective-permute-start.3 = (bf16[1,128,256]{2,1,0:T(8,128)(2,1)S(1)}, bf16[1,128,256]{2,1,0:T(8,128)(2,1)S(1)}, u32[]{:S(2)}, u32[]{:S(2)}) collective-permute-start(bf16[1,128,256]{2,1,0:T(8,128)(2,1)S(1)} %get-tuple-element.87), channel_id=1, source_target_pairs={{8,0},{12,4},{16,8},{20,12},{24,16},{28,20},{9,1},{13,5},{17,9},{2... | collective-permute-start | bytes 196616 | tf_op jit(solution)/shard_map/ppermute | solution.py:28
  81.4 8.2 %collective-permute-start.1 = (bf16[1,128,256]{2,1,0:T(8,128)(2,1)S(1)}, bf16[1,128,256]{2,1,0:T(8,128)(2,1)S(1)}, u32[]{:S(2)}, u32[]{:S(2)}) collective-permute-start(bf16[1,128,256]{2,1,0:T(8,128)(2,1)S(1)} %get-tuple-element.88), channel_id=1, source_target_pairs={{12,0},{16,4},{20,8},{24,12},{28,16},{13,1},{17,5},{21,9},{25,13},... | collective-permute-start | bytes 196616 | tf_op jit(solution)/shard_map/ppermute | solution.py:28
  82.7 27.7 %collective-permute-start.13 = (bf16[4,256,512]{2,1,0:T(8,128)(2,1)S(1)}, bf16[4,256,512]{2,1,0:T(8,128)(2,1)S(1)}, u32[]{:S(2)}, u32[]{:S(2)}) collective-permute-start(bf16[4,256,512]{2,1,0:T(8,128)(2,1)S(1)} %collective-permute-done.12), channel_id=1, source_target_pairs={{0,1},{1,2},{2,3},{3,0},{4,5},{5,6},{6,7},{7,4},{8,9},{9,10},{10,1... | collective-permute-start | bytes 3145736 | tf_op jit(solution)/shard_map/ppermute | solution.py:19
  90.0 21.1 %copy-start = (bf16[4,256,512]{2,1,0:T(8,128)(2,1)S(1)}, bf16[4,256,512]{2,1,0:T(8,128)(2,1)}, u32[]{:S(2)}) copy-start(bf16[4,256,512]{2,1,0:T(8,128)(2,1)} %param.6) | copy-start | bytes 3145732
Sparse Core Ops, SparseCore 0:
  113.1 30.2 reduce-scatter.1
